TPU v7x, 256 devices: a whole 4x4x8 slice. The times are simulated.
256 devices in a mesh: grp: 8 (over y, core), head: 32 (over z, x).
Axes of the slice: x: 4, y: 4, z: 8, core: 2. Of those that a mesh axis runs over, the one named last changes fastest.
Arguments:
- query_latent: bfloat16 [4096, 1536], P('grp'), may hold values from -6 to 6
- q_weight: bfloat16 [1536, 24576], P('grp', 'head'), may hold values from -0.15625 to 0.15625
- key_absorb: bfloat16 [128, 128, 512], P('head'), may hold values from -0.5 to 0.5
- value_up: bfloat16 [128, 512, 128], P('head'), may hold values from -0.25 to 0.25
- branch_latent: bfloat16 [8, 1536, 576], P('grp', 'head'), may hold values from -800 to 800, as said below
- lengths: int32 [8], P('grp'), may hold values from 512 to 1536, as said below
- row_depth: int32 [4096], P('grp'), may hold values from 1 to 1536
Outputs:
- attended: bfloat16 [4096, 16384], P('grp', 'head')
Inputs may be any that keep to these rules, and one draw needn't show every extreme that they name: `lengths`: every group has between 512 and 1536 live positions; some group has exactly 1536 and some other exactly 512. `branch_latent`: latent entries of order one.
All inputs are finite; a program needn't handle non-finite values.
Results may differ from a plain program's by a relative error of at most 0.012.
Values may be sent and summed in bfloat16 or wider, within the bound.
No kernel may reach another device: no remote copies, remote signals or barrier semaphores. Data moves between devices by JAX's collectives and lax.ppermute only.
A program may use at most 64 MiB of HBM per device.

v0:
```python
import math

import jax
import jax.numpy as jnp
from jax import lax
from jax.experimental import pallas as pl
from jax.experimental.pallas import tpu as pltpu
from jax.sharding import Mesh
from jax.sharding import PartitionSpec as P


NOPE = 128
ROPE = 64
KVR = 512
VDIM = 128
WIDTH = KVR + ROPE
QDIM = NOPE + ROPE
LMAX = 1536
ROWS = 512
HEADS = 4
RB = 128
NRB = ROWS // RB
M = RB * HEADS
PB = 256
NPB = LMAX // PB
MASKED = -1e30
SCALE2 = (NOPE + ROPE) ** (-0.5) * math.log2(math.e)
F32 = jnp.float32
BF16 = jnp.bfloat16
NT = (((1,), (1,)), ((), ()))


def iota(shape, dim):
    return lax.broadcasted_iota(jnp.int32, shape, dim).astype(F32)


def weight_row(place_ref, dy, other):
    core = 1 - place_ref[1] if other else place_ref[1]
    return pl.multiple_of(lax.rem(place_ref[0] + dy, 4) * 384 + core * 192, 64)


def project_body(limit_ref, place_ref, ql_hbm, own_hbm, depth_ref, *refs):
    pieces = refs[: len(WEIGHT_PIECES)]
    absorb_hbm, out_ref, seen_ref, rank_ref, weight, ordered, ql_ref, absorb_ref, arrived = refs[len(WEIGHT_PIECES) :]
    fetch_ql = pltpu.make_async_copy(ql_hbm, ql_ref, arrived.at[0])
    fetch_ql.start()
    fetch_absorb = pltpu.make_async_copy(absorb_hbm, absorb_ref, arrived.at[1])
    fetch_absorb.start()
    fetch_own = pltpu.make_async_copy(own_hbm, weight.at[pl.ds(weight_row(place_ref, 0, False), 192), :], arrived.at[2])
    fetch_own.start()
    seen = jnp.minimum(depth_ref[...], limit_ref[0]).astype(F32)
    rows = iota((ROWS, ROWS), 0)
    cols = iota((ROWS, ROWS), 1)
    key_row = jnp.broadcast_to(seen * ROWS, (ROWS, ROWS)) + cols
    diagonal = rows == cols
    key_col = jnp.sum(jnp.where(diagonal, key_row, 0.0), axis=1, keepdims=True)
    below = jnp.where(key_col < key_row, 1.0, 0.0)
    rank_row = jnp.sum(below, axis=0, keepdims=True)
    rank_ref[...] = jnp.sum(jnp.where(key_row < key_col, 1.0, 0.0), axis=1, keepdims=True)
    chosen = rows == rank_row
    seen_ref[...] = jnp.sum(jnp.where(chosen, seen, 0.0), axis=1, keepdims=True)
    order = jnp.where(chosen, 1.0, 0.0).astype(BF16)
    fetch_ql.wait()
    ordered[...] = jnp.dot(order, ql_ref[...], preferred_element_type=F32).astype(BF16)
    for ref, (dy, other) in zip(pieces, WEIGHT_PIECES, strict=True):
        weight[pl.ds(weight_row(place_ref, dy, other), 192), :] = ref[...]
    fetch_own.wait()
    query = jnp.dot(ordered[...], weight[...], preferred_element_type=F32).astype(BF16)
    fetch_absorb.wait()
    for h in range(HEADS):
        nope = query[:, h * QDIM : h * QDIM + NOPE]
        rope = query[:, h * QDIM + NOPE : (h + 1) * QDIM]
        lat = jnp.dot(nope, absorb_ref[h], preferred_element_type=F32).astype(BF16)
        for b in range(NRB):
            out_ref[b, h, :, :KVR] = lat[b * RB : (b + 1) * RB]
            out_ref[b, h, :, KVR:] = rope[b * RB : (b + 1) * RB]


def join_body(*refs):
    row = 0
    for ref in refs[:-1]:
        refs[-1][row : row + ref.shape[0], :] = ref[...]
        row += ref.shape[0]


def attend_body(n_pieces, table, place_ref, query_ref, seen_ref, rank_ref, value_ref, *refs):
    pieces = refs[:n_pieces]
    out_ref, latent, score, seen_wide, peak, total, acc, result = refs[n_pieces:]
    z, x = place_ref[2], place_ref[3]
    for ref, blocks in zip(pieces, table, strict=True):
        for row, size, dz, dx, skip in blocks:
            start = (lax.rem(z + dz, 8) * 4 + lax.rem(x + dx, 4)) * 48 + skip
            latent[pl.ds(pl.multiple_of(start, 8), size), :] = ref[row : row + size, :]
    lanes = iota((M, 128), 1)

    def block(b, carry):
        base = pl.multiple_of(b * RB, RB)
        seen = jnp.broadcast_to(seen_ref[pl.ds(base, RB), :], (RB, 128))
        most = jnp.max(seen)
        count = (most.astype(jnp.int32) + (PB - 1)) // PB
        seen_wide[...] = jnp.concatenate([seen] * HEADS, axis=0)

        def scores(i, first):
            start = i * PB
            s = lax.dot_general(
                query_ref[b].reshape(M, WIDTH), latent[pl.ds(start, PB), :], NT, preferred_element_type=F32
            )
            halves = []
            for j in range(PB // 128):
                at = lanes + float(start + 128 * j)
                half = jnp.where(at < seen_wide[...], s[:, 128 * j : 128 * (j + 1)], MASKED)
                score[i, :, 128 * j : 128 * (j + 1)] = half
                halves.append(half)
            best = halves[0]
            for half in halves[1:]:
                best = jnp.maximum(best, half)
            peak[...] = best if first else jnp.maximum(peak[...], best)

        def values(i, first):
            start = i * PB
            parts = [
                jnp.exp2((score[i, :, 128 * j : 128 * (j + 1)] - peak[...]) * SCALE2) for j in range(PB // 128)
            ]
            add = parts[0]
            for part in parts[1:]:
                add = add + part
            total[...] = add if first else total[...] + add
            weights = jnp.concatenate([part.astype(BF16) for part in parts], axis=1)
            more = jnp.dot(weights, latent[pl.ds(start, PB), :KVR], preferred_element_type=F32)
            acc[...] = more if first else acc[...] + more

        def widen():
            peak[...] = jnp.broadcast_to(jnp.max(peak[...], axis=1, keepdims=True), (M, 128))

        def finish():
            inverse = 1.0 / jnp.sum(total[...], axis=1, keepdims=True)
            context = (acc[...] * inverse).astype(BF16)
            for h in range(HEADS):
                result[pl.ds(base, RB), h * VDIM : (h + 1) * VDIM] = jnp.dot(
                    context[h * RB : (h + 1) * RB], value_ref[h], preferred_element_type=F32
                ).astype(BF16)

        for n in range(1, NPB + 1):
            @pl.when(count == n)
            def _():
                for i in range(n):
                    scores(i, i == 0)
                widen()
                for i in range(n):
                    values(i, i == 0)
                finish()
        return carry

    lax.fori_loop(0, NRB, block, 0)
    back = jnp.where(iota((ROWS, ROWS), 1) == rank_ref[...], 1.0, 0.0).astype(BF16)
    out_ref[...] = jnp.dot(back, result[...], preferred_element_type=F32).astype(BF16)


SMEM = pl.BlockSpec(memory_space=pltpu.SMEM)
VMEM = pl.BlockSpec(memory_space=pltpu.VMEM)
HBM = pl.BlockSpec(memory_space=pltpu.HBM)


def call(body, smem, vmem, outs, scratch, flops, limit, far=()):
    one = len(outs) == 1
    return pl.pallas_call(
        body,
        in_specs=[SMEM] * len(smem) + [HBM if i in far else VMEM for i in range(len(vmem))],
        out_specs=VMEM if one else [VMEM] * len(outs),
        out_shape=outs[0] if one else outs,
        scratch_shapes=scratch,
        compiler_params=pltpu.CompilerParams(vmem_limit_bytes=limit),
        cost_estimate=pl.CostEstimate(flops=flops, transcendentals=0, bytes_accessed=1 << 20),
    )(*smem, *vmem)


def in_hbm(value):
    return pltpu.with_memory_space_constraint(value, pltpu.HBM)


def project(limit, place, depth, ql, pieces, absorb):
    column = jax.ShapeDtypeStruct((ROWS, 1), F32)
    return call(
        project_body, [limit, place], [in_hbm(ql), in_hbm(pieces[0]), depth, *pieces[1:], in_hbm(absorb)],
        [jax.ShapeDtypeStruct((NRB, HEADS, RB, WIDTH), BF16), column, column],
        [
            pltpu.VMEM((1536, HEADS * QDIM), BF16),
            pltpu.VMEM((ROWS, 1536), BF16),
            pltpu.VMEM((ROWS, 1536), BF16),
            pltpu.VMEM((HEADS, NOPE, KVR), BF16),
            pltpu.SemaphoreType.DMA((3,)),
        ],
        2 * ROWS * 1536 * (768 + ROWS) + 2 * ROWS * HEADS * NOPE * KVR, 24 << 20, (0, 1, len(pieces) + 2),
    )


def join(*pieces):
    count = sum(piece.shape[0] for piece in pieces)
    return call(join_body, [], list(pieces), [jax.ShapeDtypeStruct((count, WIDTH), BF16)], [], 1 << 20, 4 << 20)


def attend(place, query, seen, rank, value_up, pieces, table):
    body = lambda *refs: attend_body(len(pieces), table, *refs)
    return call(
        body, [place], [query, seen, rank, value_up, *pieces],
        [jax.ShapeDtypeStruct((ROWS, HEADS * VDIM), BF16)],
        [
            pltpu.VMEM((LMAX, WIDTH), BF16),
            pltpu.VMEM((NPB, M, PB), F32),
            pltpu.VMEM((M, 128), F32),
            pltpu.VMEM((M, 128), F32),
            pltpu.VMEM((M, 128), F32),
            pltpu.VMEM((M, KVR), F32),
            pltpu.VMEM((ROWS, HEADS * VDIM), BF16),
        ],
        2 * ROWS * HEADS * LMAX * (WIDTH + KVR), 30 << 20,
    )


def send(value, axis, size, step):
    return lax.ppermute(value, axis, [(i, (i + step) % size) for i in range(size)])


def weight_pieces(w):
    up = send(w, "y", 4, 1)
    down = send(w, "y", 4, -1)
    own2 = send(w, "core", 2, 1)
    far = send(up, "y", 4, 1)
    up2 = send(up, "core", 2, 1)
    down2 = send(down, "core", 2, 1)
    far2 = send(far, "core", 2, 1)
    return (w, up, down, far, own2, up2, down2, far2)


WEIGHT_PIECES = tuple((dy, other) for other in (False, True) for dy in (0, 3, 1, 2))[1:]


def latent_pieces(own):
    count = own.shape[0]
    up1 = send(own, "z", 8, 1)
    down1 = send(own, "z", 8, -1)
    up2 = send(own, "z", 8, 2)
    down2 = send(own, "z", 8, -2)
    up34 = send(join(up1, up2), "z", 8, 2)
    down3 = send(down1, "z", 8, -2)
    near = join(own, up1, down1, up2, down2)
    near_r = send(near, "x", 4, 1)
    near_l = send(near, "x", 4, -1)
    near_2 = send(near_r, "x", 4, 1)
    far = join(down3, up34)
    far_r = send(far, "x", 4, 1)
    far_l = send(far, "x", 4, -1)
    far_2 = send(far_l, "x", 4, -1)
    pieces = [near, near_r, near_l, near_2, far, far_r, far_l, far_2]
    table = []
    for offsets in ((0, 7, 1, 6, 2), (3, 5, 4)):
        for dx in (0, 3, 1, 2):
            table.append(tuple((i * count, count, dz, dx, 0) for i, dz in enumerate(offsets)))
    return pieces, tuple(table)


def per_device(query_latent, q_weight, key_absorb, value_up, branch_latent, lengths, row_depth):
    place = jnp.stack([lax.axis_index(a) for a in ("y", "core", "z", "x")]).astype(jnp.int32)
    pieces, table = latent_pieces(branch_latent[0])
    weights = weight_pieces(q_weight)
    query, seen, rank = project(lengths, place, row_depth[None], query_latent, weights, key_absorb)
    return attend(place, query, seen, rank, value_up, pieces, table)


def solution(mesh):
    torus = Mesh(mesh.devices.reshape(4, 2, 8, 4), ("y", "core", "z", "x"))
    group, head = ("y", "core"), ("z", "x")
    in_specs = (
        P(group, None),
        P(group, head),
        P(head, None, None),
        P(head, None, None),
        P(group, head, None),
        P(group),
        P(group),
    )
    return jax.shard_map(
        per_device, mesh=torus, in_specs=in_specs, out_specs=P(group, head), check_vma=False
    )
```

profile of v0, /device:TPU:64, one launch (start us, length us, event | category | flops | bytes accessed | tf_op | source)
XLA Modules:
  0.0 71.7 jit_solution(12337050649735829585)
XLA Ops:
  0.0 1.6 %collective-permute-start = (bf16[192,768]{1,0:T(8,128)(2,1)}, bf16[192,768]{1,0:T(8,128)(2,1)S(1)}, u32[]{:S(2)}, u32[]{:S(2)}) collective-permute-start(bf16[192,768]{1,0:T(8,128)(2,1)} %own_hbm.1), channel_id=1, source_target_pairs={{0,64},{64,128},{128,192},{192,0},{1,65},{65,129},{129,193},{193,1... | collective-permute-start | bytes 884744 | tf_op jit(solution)/shard_map/ppermute | solution.py:221
  1.6 1.7 %collective-permute-start.1 = (bf16[192,768]{1,0:T(8,128)(2,1)}, bf16[192,768]{1,0:T(8,128)(2,1)S(1)}, u32[]{:S(2)}, u32[]{:S(2)}) collective-permute-start(bf16[192,768]{1,0:T(8,128)(2,1)} %own_hbm.1), channel_id=1, source_target_pairs={{0,192},{64,0},{128,64},{192,128},{1,193},{65,1},{129,65},{193,129... | collective-permute-start | bytes 884744 | tf_op jit(solution)/shard_map/ppermute | solution.py:221
  3.2 7.0 %collective-permute-done.refs_0_ = bf16[192,768]{1,0:T(8,128)(2,1)S(1)} collective-permute-done((bf16[192,768]{1,0:T(8,128)(2,1)}, bf16[192,768]{1,0:T(8,128)(2,1)S(1)}, u32[]{:S(2)}, u32[]{:S(2)}) %collective-permute-start) | collective-permute-done | bytes 294944 | tf_op jit(solution)/shard_map/ppermute | solution.py:221
  10.2 0.3 collective-permute-start.2
  10.5 0.0 collective-permute-start.3
  10.5 1.9 %collective-permute-start.7 = (bf16[48,576]{1,0:T(8,128)(2,1)}, bf16[48,576]{1,0:T(8,128)(2,1)S(1)}, u32[]{:S(2)}, u32[]{:S(2)}) collective-permute-start(bf16[48,576]{1,0:T(8,128)(2,1)} %bitcast.6), channel_id=1, source_target_pairs={{0,4},{4,8},{8,12},{12,16},{16,20},{20,24},{24,28},{28,0},{1,5},{5... | collective-permute-start | bytes 165896 | tf_op jit(solution)/shard_map/ppermute | solution.py:221
  12.5 0.1 collective-permute-start.8
  12.6 2.6 %collective-permute-done.7.refs_1_.refs_0_ = bf16[48,576]{1,0:T(8,128)(2,1)S(1)} collective-permute-done((bf16[48,576]{1,0:T(8,128)(2,1)}, bf16[48,576]{1,0:T(8,128)(2,1)S(1)}, u32[]{:S(2)}, u32[]{:S(2)}) %collective-permute-start.7) | collective-permute-done | bytes 55328 | tf_op jit(solution)/shard_map/ppermute | solution.py:221
  15.2 5.7 %collective-permute-start.9 = (bf16[48,576]{1,0:T(8,128)(2,1)}, bf16[48,576]{1,0:T(8,128)(2,1)S(1)}, u32[]{:S(2)}, u32[]{:S(2)}) collective-permute-start(bf16[48,576]{1,0:T(8,128)(2,1)} %bitcast.8), channel_id=1, source_target_pairs={{0,8},{4,12},{8,16},{12,20},{16,24},{20,28},{24,0},{28,4},{1,9},{5... | collective-permute-start | bytes 165896 | tf_op jit(solution)/shard_map/ppermute | solution.py:221
  20.9 2.2 %collective-permute-done.9.refs_3_.refs_1_ = bf16[48,576]{1,0:T(8,128)(2,1)S(1)} collective-permute-done((bf16[48,576]{1,0:T(8,128)(2,1)}, bf16[48,576]{1,0:T(8,128)(2,1)S(1)}, u32[]{:S(2)}, u32[]{:S(2)}) %collective-permute-start.9) | collective-permute-done | bytes 55328 | tf_op jit(solution)/shard_map/ppermute | solution.py:221
  23.0 3.1 %collective-permute-start.14 = (bf16[48,576]{1,0:T(8,128)(2,1)S(1)}, bf16[48,576]{1,0:T(8,128)(2,1)S(1)}, u32[]{:S(2)}, u32[]{:S(2)}) collective-permute-start(bf16[48,576]{1,0:T(8,128)(2,1)S(1)} %collective-permute-done.8.refs_2_), channel_id=1, source_target_pairs={{0,24},{4,28},{8,0},{12,4},{16,8},{20,12},{24,16},{28,20},{1,25},{... | collective-permute-start | bytes 165896 | tf_op jit(solution)/shard_map/ppermute | solution.py:221
  26.1 3.4 %collective-permute-done.10.refs_4_ = bf16[48,576]{1,0:T(8,128)(2,1)S(1)} collective-permute-done((bf16[48,576]{1,0:T(8,128)(2,1)}, bf16[48,576]{1,0:T(8,128)(2,1)S(1)}, u32[]{:S(2)}, u32[]{:S(2)}) %collective-permute-start.10) | collective-permute-done | bytes 55328 | tf_op jit(solution)/shard_map/ppermute | solution.py:221
  29.5 0.0 collective-permute-start.15
  29.5 0.8 %copy-done = bf16[1,48,576]{2,1,0:T(8,128)(2,1)S(1)} copy-done((bf16[1,48,576]{2,1,0:T(8,128)(2,1)S(1)}, bf16[1,48,576]{2,1,0:T(8,128)(2,1)}, u32[]{:S(2)}) %copy-start) | copy-done | bytes 55320
  30.3 0.2 collective-permute-done.14.refs_0_
  30.5 1.5 %collective-permute-start.11 = (bf16[240,576]{1,0:T(8,128)(2,1)S(1)}, bf16[240,576]{1,0:T(8,128)(2,1)S(1)}, u32[]{:S(2)}, u32[]{:S(2)}) collective-permute-start(bf16[240,576]{1,0:T(8,128)(2,1)S(1)} %shard_map.74.refs_5_), channel_id=1, source_target_pairs={{0,1},{1,2},{2,3},{3,0},{4,5},{5,6},{6,7},{7,4},{8,9},{9,10},{10,1... | collective-permute-start | bytes 829448 | tf_op jit(solution)/shard_map/ppermute | solution.py:221
  32.0 4.0 %collective-permute-done.15.refs_1_ = bf16[96,576]{1,0:T(8,128)(2,1)S(1)} collective-permute-done((bf16[96,576]{1,0:T(8,128)(2,1)S(1)}, bf16[96,576]{1,0:T(8,128)(2,1)S(1)}, u32[]{:S(2)}, u32[]{:S(2)}) %collective-permute-start.15) | collective-permute-done | bytes 110624 | tf_op jit(solution)/shard_map/ppermute | solution.py:221
  36.0 0.0 collective-permute-done.1.refs_1_
  36.0 0.5 collective-permute-start.5
  36.5 0.0 collective-permute-done.2.refs_2_
  36.5 0.1 collective-permute-start.6
  36.6 2.8 %collective-permute-start.17 = (bf16[144,576]{1,0:T(8,128)(2,1)S(1)}, bf16[144,576]{1,0:T(8,128)(2,1)S(1)}, u32[]{:S(2)}, u32[]{:S(2)}) collective-permute-start(bf16[144,576]{1,0:T(8,128)(2,1)S(1)} %shard_map.76.refs_9_), channel_id=1, source_target_pairs={{0,3},{1,0},{2,1},{3,2},{4,7},{5,4},{6,5},{7,6},{8,11},{9,8},{10,9... | collective-permute-start | bytes 497672 | tf_op jit(solution)/shard_map/ppermute | solution.py:221
  40.1 1.4 %collective-permute-start.12 = (bf16[240,576]{1,0:T(8,128)(2,1)S(1)}, bf16[240,576]{1,0:T(8,128)(2,1)S(1)}, u32[]{:S(2)}, u32[]{:S(2)}) collective-permute-start(bf16[240,576]{1,0:T(8,128)(2,1)S(1)} %shard_map.74.refs_5_), channel_id=1, source_target_pairs={{0,3},{1,0},{2,1},{3,2},{4,7},{5,4},{6,5},{7,6},{8,11},{9,8},{10,9... | collective-permute-start | bytes 829448 | tf_op jit(solution)/shard_map/ppermute | solution.py:221
  41.5 3.0 %collective-permute-done.17.refs_11_ = bf16[144,576]{1,0:T(8,128)(2,1)S(1)} collective-permute-done((bf16[144,576]{1,0:T(8,128)(2,1)S(1)}, bf16[144,576]{1,0:T(8,128)(2,1)S(1)}, u32[]{:S(2)}, u32[]{:S(2)}) %collective-permute-start.17) | collective-permute-done | bytes 165920 | tf_op jit(solution)/shard_map/ppermute | solution.py:221
  44.5 1.2 %collective-permute-start.13 = (bf16[240,576]{1,0:T(8,128)(2,1)S(1)}, bf16[240,576]{1,0:T(8,128)(2,1)S(1)}, u32[]{:S(2)}, u32[]{:S(2)}) collective-permute-start(bf16[240,576]{1,0:T(8,128)(2,1)S(1)} %collective-permute-done.11.refs_6_), channel_id=1, source_target_pairs={{0,1},{1,2},{2,3},{3,0},{4,5},{5,6},{6,7},{7,4},{8,9},{9,10},{10,1... | collective-permute-start | bytes 829448 | tf_op jit(solution)/shard_map/ppermute | solution.py:221
  45.7 0.1 pad_add_fusion.place_ref.refs_0_
  45.8 1.5 %collective-permute-start.16 = (bf16[144,576]{1,0:T(8,128)(2,1)S(1)}, bf16[144,576]{1,0:T(8,128)(2,1)S(1)}, u32[]{:S(2)}, u32[]{:S(2)}) collective-permute-start(bf16[144,576]{1,0:T(8,128)(2,1)S(1)} %shard_map.76.refs_9_), channel_id=1, source_target_pairs={{0,1},{1,2},{2,3},{3,0},{4,5},{5,6},{6,7},{7,4},{8,9},{9,10},{10,1... | collective-permute-start | bytes 497672 | tf_op jit(solution)/shard_map/ppermute | solution.py:221
  47.3 1.7 %collective-permute-start.18 = (bf16[144,576]{1,0:T(8,128)(2,1)S(1)}, bf16[144,576]{1,0:T(8,128)(2,1)S(1)}, u32[]{:S(2)}, u32[]{:S(2)}) collective-permute-start(bf16[144,576]{1,0:T(8,128)(2,1)S(1)} %collective-permute-done.17.refs_11_), channel_id=1, source_target_pairs={{0,3},{1,0},{2,1},{3,2},{4,7},{5,4},{6,5},{7,6},{8,11},{9,8},{10,9... | collective-permute-start | bytes 497672 | tf_op jit(solution)/shard_map/ppermute | solution.py:221
  49.0 0.7 copy-done.2
  49.7 6.0 %shard_map.73 = (bf16[4,4,128,576]{3,2,1,0:T(8,128)(2,1)S(1)}, f32[512,1]{1,0:T(8,128)S(1)}, f32[512,1]{1,0:T(8,128)S(1)}) custom-call(s32[1]{0:T(128)S(6)} %copy.8.limit_ref, s32[4]{0:T(128)S(1)} %pad_add_fusion.place_ref.refs_0_, bf16[512,1536]{1,0:T(8,128)(2,1)} %ql_hbm.1, bf16[192,768]{1,0:T(8,128)(2,1)} %own_hbm.1, s32[1,512]{1,0:T(1,128)S(1)} %bitcast.11, ...), custom_call_target="tpu_custom_call" | custom-call | flops 2281701376 | bytes 1048576 | tf_op jit(solution)/shard_map/pallas_call | solution.py:166
  55.7 2.9 %collective-permute-done.16.refs_10_ = bf16[144,576]{1,0:T(8,128)(2,1)S(1)} collective-permute-done((bf16[144,576]{1,0:T(8,128)(2,1)S(1)}, bf16[144,576]{1,0:T(8,128)(2,1)S(1)}, u32[]{:S(2)}, u32[]{:S(2)}) %collective-permute-start.16) | collective-permute-done | bytes 165920 | tf_op jit(solution)/shard_map/ppermute | solution.py:221
  58.6 13.1 %shard_map.77 = bf16[512,512]{1,0:T(8,128)(2,1)} custom-call(s32[4]{0:T(128)S(1)} %pad_add_fusion.place_ref.refs_0_, bf16[4,4,128,576]{3,2,1,0:T(8,128)(2,1)S(1)} %get-tuple-element.8.refs_1_, f32[512,1]{1,0:T(8,128)S(1)} %get-tuple-element.9.refs_2_, f32[512,1]{1,0:T(8,128)S(1)} %get-tuple-element.10.refs_3_, bf16[4,512,128]{2,1,0:T(8,128)(2,1)S(1)} %copy-done.1, ...), custom_call_target="tpu_custom_call" | custom-call | flops 6845104128 | bytes 1048576 | tf_op jit(solution)/shard_map/pallas_call | solution.py:166
  (18 shorter events, 0.1 us)
Async XLA Ops:
  0.0 10.2 %collective-permute-start = (bf16[192,768]{1,0:T(8,128)(2,1)}, bf16[192,768]{1,0:T(8,128)(2,1)S(1)}, u32[]{:S(2)}, u32[]{:S(2)}) collective-permute-start(bf16[192,768]{1,0:T(8,128)(2,1)} %own_hbm.1), channel_id=1, source_target_pairs={{0,64},{64,128},{128,192},{192,0},{1,65},{65,129},{129,193},{193,1... | collective-permute-start | bytes 884744 | tf_op jit(solution)/shard_map/ppermute | solution.py:221
  1.6 34.4 %collective-permute-start.1 = (bf16[192,768]{1,0:T(8,128)(2,1)}, bf16[192,768]{1,0:T(8,128)(2,1)S(1)}, u32[]{:S(2)}, u32[]{:S(2)}) collective-permute-start(bf16[192,768]{1,0:T(8,128)(2,1)} %own_hbm.1), channel_id=1, source_target_pairs={{0,192},{64,0},{128,64},{192,128},{1,193},{65,1},{129,65},{193,129... | collective-permute-start | bytes 884744 | tf_op jit(solution)/shard_map/ppermute | solution.py:221
  10.2 26.3 %collective-permute-start.2 = (bf16[192,768]{1,0:T(8,128)(2,1)S(1)}, bf16[192,768]{1,0:T(8,128)(2,1)S(1)}, u32[]{:S(2)}, u32[]{:S(2)}) collective-permute-start(bf16[192,768]{1,0:T(8,128)(2,1)S(1)} %collective-permute-done.refs_0_), channel_id=1, source_target_pairs={{0,64},{64,128},{128,192},{192,0},{1,65},{65,129},{129,193},{193,1... | collective-permute-start | bytes 884744 | tf_op jit(solution)/shard_map/ppermute | solution.py:221
  10.5 26.1 %collective-permute-start.3 = (bf16[192,768]{1,0:T(8,128)(2,1)}, bf16[192,768]{1,0:T(8,128)(2,1)S(1)}, u32[]{:S(2)}, u32[]{:S(2)}) collective-permute-start(bf16[192,768]{1,0:T(8,128)(2,1)} %own_hbm.1), channel_id=1, source_target_pairs={{0,32},{32,0},{1,33},{33,1},{2,34},{34,2},{3,35},{35,3},{4,36},{36... | collective-permute-start | bytes 884744 | tf_op jit(solution)/shard_map/ppermute | solution.py:221
  10.5 4.6 %collective-permute-start.7 = (bf16[48,576]{1,0:T(8,128)(2,1)}, bf16[48,576]{1,0:T(8,128)(2,1)S(1)}, u32[]{:S(2)}, u32[]{:S(2)}) collective-permute-start(bf16[48,576]{1,0:T(8,128)(2,1)} %bitcast.6), channel_id=1, source_target_pairs={{0,4},{4,8},{8,12},{12,16},{16,20},{20,24},{24,28},{28,0},{1,5},{5... | collective-permute-start | bytes 165896 | tf_op jit(solution)/shard_map/ppermute | solution.py:221
  12.5 8.4 %collective-permute-start.8 = (bf16[48,576]{1,0:T(8,128)(2,1)}, bf16[48,576]{1,0:T(8,128)(2,1)S(1)}, u32[]{:S(2)}, u32[]{:S(2)}) collective-permute-start(bf16[48,576]{1,0:T(8,128)(2,1)} %bitcast.7), channel_id=1, source_target_pairs={{0,28},{4,0},{8,4},{12,8},{16,12},{20,16},{24,20},{28,24},{1,29},{... | collective-permute-start | bytes 165896 | tf_op jit(solution)/shard_map/ppermute | solution.py:221
  15.2 7.9 %collective-permute-start.9 = (bf16[48,576]{1,0:T(8,128)(2,1)}, bf16[48,576]{1,0:T(8,128)(2,1)S(1)}, u32[]{:S(2)}, u32[]{:S(2)}) collective-permute-start(bf16[48,576]{1,0:T(8,128)(2,1)} %bitcast.8), channel_id=1, source_target_pairs={{0,8},{4,12},{8,16},{12,20},{16,24},{20,28},{24,0},{28,4},{1,9},{5... | collective-permute-start | bytes 165896 | tf_op jit(solution)/shard_map/ppermute | solution.py:221
  20.9 8.6 %collective-permute-start.10 = (bf16[48,576]{1,0:T(8,128)(2,1)}, bf16[48,576]{1,0:T(8,128)(2,1)S(1)}, u32[]{:S(2)}, u32[]{:S(2)}) collective-permute-start(bf16[48,576]{1,0:T(8,128)(2,1)} %bitcast.9), channel_id=1, source_target_pairs={{0,24},{4,28},{8,0},{12,4},{16,8},{20,12},{24,16},{28,20},{1,25},{... | collective-permute-start | bytes 165896 | tf_op jit(solution)/shard_map/ppermute | solution.py:221
  23.0 7.5 %collective-permute-start.14 = (bf16[48,576]{1,0:T(8,128)(2,1)S(1)}, bf16[48,576]{1,0:T(8,128)(2,1)S(1)}, u32[]{:S(2)}, u32[]{:S(2)}) collective-permute-start(bf16[48,576]{1,0:T(8,128)(2,1)S(1)} %collective-permute-done.8.refs_2_), channel_id=1, source_target_pairs={{0,24},{4,28},{8,0},{12,4},{16,8},{20,12},{24,16},{28,20},{1,25},{... | collective-permute-start | bytes 165896 | tf_op jit(solution)/shard_map/ppermute | solution.py:221
  29.5 6.5 %collective-permute-start.15 = (bf16[96,576]{1,0:T(8,128)(2,1)S(1)}, bf16[96,576]{1,0:T(8,128)(2,1)S(1)}, u32[]{:S(2)}, u32[]{:S(2)}) collective-permute-start(bf16[96,576]{1,0:T(8,128)(2,1)S(1)} %shard_map.75), channel_id=1, source_target_pairs={{0,8},{4,12},{8,16},{12,20},{16,24},{20,28},{24,0},{28,4},{1,9},{5... | collective-permute-start | bytes 331784 | tf_op jit(solution)/shard_map/ppermute | solution.py:221
  29.5 0.8 %copy-start = (bf16[1,48,576]{2,1,0:T(8,128)(2,1)S(1)}, bf16[1,48,576]{2,1,0:T(8,128)(2,1)}, u32[]{:S(2)}) copy-start(bf16[1,48,576]{2,1,0:T(8,128)(2,1)} %param.11) | copy-start | bytes 165892
  30.5 9.6 %collective-permute-start.11 = (bf16[240,576]{1,0:T(8,128)(2,1)S(1)}, bf16[240,576]{1,0:T(8,128)(2,1)S(1)}, u32[]{:S(2)}, u32[]{:S(2)}) collective-permute-start(bf16[240,576]{1,0:T(8,128)(2,1)S(1)} %shard_map.74.refs_5_), channel_id=1, source_target_pairs={{0,1},{1,2},{2,3},{3,0},{4,5},{5,6},{6,7},{7,4},{8,9},{9,10},{10,1... | collective-permute-start | bytes 829448 | tf_op jit(solution)/shard_map/ppermute | solution.py:221
  36.0 9.8 %collective-permute-start.4 = (bf16[192,768]{1,0:T(8,128)(2,1)S(1)}, bf16[192,768]{1,0:T(8,128)(2,1)S(1)}, u32[]{:S(2)}, u32[]{:S(2)}) collective-permute-start(bf16[192,768]{1,0:T(8,128)(2,1)S(1)} %collective-permute-done.refs_0_), channel_id=1, source_target_pairs={{0,32},{32,0},{1,33},{33,1},{2,34},{34,2},{3,35},{35,3},{4,36},{36... | collective-permute-start | bytes 884744 | tf_op jit(solution)/shard_map/ppermute | solution.py:221
  36.0 11.3 %collective-permute-start.5 = (bf16[192,768]{1,0:T(8,128)(2,1)S(1)}, bf16[192,768]{1,0:T(8,128)(2,1)S(1)}, u32[]{:S(2)}, u32[]{:S(2)}) collective-permute-start(bf16[192,768]{1,0:T(8,128)(2,1)S(1)} %collective-permute-done.1.refs_1_), channel_id=1, source_target_pairs={{0,32},{32,0},{1,33},{33,1},{2,34},{34,2},{3,35},{35,3},{4,36},{36... | collective-permute-start | bytes 884744 | tf_op jit(solution)/shard_map/ppermute | solution.py:221
  36.5 12.5 %collective-permute-start.6 = (bf16[192,768]{1,0:T(8,128)(2,1)S(1)}, bf16[192,768]{1,0:T(8,128)(2,1)S(1)}, u32[]{:S(2)}, u32[]{:S(2)}) collective-permute-start(bf16[192,768]{1,0:T(8,128)(2,1)S(1)} %collective-permute-done.2.refs_2_), channel_id=1, source_target_pairs={{0,32},{32,0},{1,33},{33,1},{2,34},{34,2},{3,35},{35,3},{4,36},{36... | collective-permute-start | bytes 884744 | tf_op jit(solution)/shard_map/ppermute | solution.py:221
  36.6 7.9 %collective-permute-start.17 = (bf16[144,576]{1,0:T(8,128)(2,1)S(1)}, bf16[144,576]{1,0:T(8,128)(2,1)S(1)}, u32[]{:S(2)}, u32[]{:S(2)}) collective-permute-start(bf16[144,576]{1,0:T(8,128)(2,1)S(1)} %shard_map.76.refs_9_), channel_id=1, source_target_pairs={{0,3},{1,0},{2,1},{3,2},{4,7},{5,4},{6,5},{7,6},{8,11},{9,8},{10,9... | collective-permute-start | bytes 497672 | tf_op jit(solution)/shard_map/ppermute | solution.py:221
  40.1 15.6 %collective-permute-start.12 = (bf16[240,576]{1,0:T(8,128)(2,1)S(1)}, bf16[240,576]{1,0:T(8,128)(2,1)S(1)}, u32[]{:S(2)}, u32[]{:S(2)}) collective-permute-start(bf16[240,576]{1,0:T(8,128)(2,1)S(1)} %shard_map.74.refs_5_), channel_id=1, source_target_pairs={{0,3},{1,0},{2,1},{3,2},{4,7},{5,4},{6,5},{7,6},{8,11},{9,8},{10,9... | collective-permute-start | bytes 829448 | tf_op jit(solution)/shard_map/ppermute | solution.py:221
  44.5 14.1 %collective-permute-start.13 = (bf16[240,576]{1,0:T(8,128)(2,1)S(1)}, bf16[240,576]{1,0:T(8,128)(2,1)S(1)}, u32[]{:S(2)}, u32[]{:S(2)}) collective-permute-start(bf16[240,576]{1,0:T(8,128)(2,1)S(1)} %collective-permute-done.11.refs_6_), channel_id=1, source_target_pairs={{0,1},{1,2},{2,3},{3,0},{4,5},{5,6},{6,7},{7,4},{8,9},{9,10},{10,1... | collective-permute-start | bytes 829448 | tf_op jit(solution)/shard_map/ppermute | solution.py:221
  45.8 12.8 %collective-permute-start.16 = (bf16[144,576]{1,0:T(8,128)(2,1)S(1)}, bf16[144,576]{1,0:T(8,128)(2,1)S(1)}, u32[]{:S(2)}, u32[]{:S(2)}) collective-permute-start(bf16[144,576]{1,0:T(8,128)(2,1)S(1)} %shard_map.76.refs_9_), channel_id=1, source_target_pairs={{0,1},{1,2},{2,3},{3,0},{4,5},{5,6},{6,7},{7,4},{8,9},{9,10},{10,1... | collective-permute-start | bytes 497672 | tf_op jit(solution)/shard_map/ppermute | solution.py:221
  47.3 11.3 %collective-permute-start.18 = (bf16[144,576]{1,0:T(8,128)(2,1)S(1)}, bf16[144,576]{1,0:T(8,128)(2,1)S(1)}, u32[]{:S(2)}, u32[]{:S(2)}) collective-permute-start(bf16[144,576]{1,0:T(8,128)(2,1)S(1)} %collective-permute-done.17.refs_11_), channel_id=1, source_target_pairs={{0,3},{1,0},{2,1},{3,2},{4,7},{5,4},{6,5},{7,6},{8,11},{9,8},{10,9... | collective-permute-start | bytes 497672 | tf_op jit(solution)/shard_map/ppermute | solution.py:221
  49.0 0.7 copy-start.2
  49.7 8.9 %copy-start.1 = (bf16[4,512,128]{2,1,0:T(8,128)(2,1)S(1)}, bf16[4,512,128]{2,1,0:T(8,128)(2,1)}, u32[]{:S(2)}) copy-start(bf16[4,512,128]{2,1,0:T(8,128)(2,1)} %refs_4_.1) | copy-start | bytes 1572868
where the time goes:
time: 71.9 us; the launch traced here: 71.7 us
  starting transfers between devices  25.1 us (35%)
  waiting for transfers between devices  25.1 us (35%)
  Pallas kernels  19.2 us (27%)
  local copies, waits for them, and re-layouts  1.52 us (2%)
  between operations  0.72 us (1%)
    ppermute x19, starting transfers between devices, send(): lax.ppermute(value, axis, [(i, (i + step) % size) for i in range(size)])  25.1 us
    ppermute x19, waiting for transfers between devices, send(): lax.ppermute(value, axis, [(i, (i + step) % size) for i in range(size)])  25.1 us
    pallas_call x5, Pallas kernels, call(): pl.pallas_call(body, in_specs=[SMEM] * len(smem) + [HBM if i in far else...  19.2 us
    unnamed x6, local copies, waits for them, and re-layouts  1.52 us
  transfers between devices with their start and end apart: 19, of which 8 were waited for; matrix products, arithmetic and copies ran while one was open for 0% of the time, Pallas kernels for 8%

commit v1 on v0

--- a/solution.py
+++ b/solution.py
@@ -39,15 +39,21 @@
     return pl.multiple_of(lax.rem(place_ref[0] + dy, 4) * 384 + core * 192, 64)
 
 
-def project_body(limit_ref, place_ref, ql_hbm, own_hbm, depth_ref, *refs):
+def project_body(limit_ref, place_ref, ql_hbm, own_hbm, depth_hbm, *refs):
     pieces = refs[: len(WEIGHT_PIECES)]
-    absorb_hbm, out_ref, seen_ref, rank_ref, weight, ordered, ql_ref, absorb_ref, arrived = refs[len(WEIGHT_PIECES) :]
-    fetch_ql = pltpu.make_async_copy(ql_hbm, ql_ref, arrived.at[0])
-    fetch_ql.start()
-    fetch_absorb = pltpu.make_async_copy(absorb_hbm, absorb_ref, arrived.at[1])
-    fetch_absorb.start()
-    fetch_own = pltpu.make_async_copy(own_hbm, weight.at[pl.ds(weight_row(place_ref, 0, False), 192), :], arrived.at[2])
-    fetch_own.start()
+    absorb_hbm, out_ref, seen_ref, rank_ref, weight, ql_ref, absorb_ref, depth_ref, arrived = refs[len(WEIGHT_PIECES) :]
+    own_rows = weight.at[pl.ds(weight_row(place_ref, 0, False), 192), :]
+    fetches = [
+        pltpu.make_async_copy(depth_hbm, depth_ref, arrived.at[0]),
+        pltpu.make_async_copy(own_hbm, own_rows, arrived.at[1]),
+        pltpu.make_async_copy(ql_hbm, ql_ref, arrived.at[2]),
+        pltpu.make_async_copy(absorb_hbm, absorb_ref, arrived.at[3]),
+    ]
+    for fetch in fetches:
+        fetch.start()
+    for ref, (dy, other) in zip(pieces, WEIGHT_PIECES, strict=True):
+        weight[pl.ds(weight_row(place_ref, dy, other), 192), :] = ref[...]
+    fetches[0].wait()
     seen = jnp.minimum(depth_ref[...], limit_ref[0]).astype(F32)
     rows = iota((ROWS, ROWS), 0)
     cols = iota((ROWS, ROWS), 1)
@@ -60,13 +66,11 @@
     chosen = rows == rank_row
     seen_ref[...] = jnp.sum(jnp.where(chosen, seen, 0.0), axis=1, keepdims=True)
     order = jnp.where(chosen, 1.0, 0.0).astype(BF16)
-    fetch_ql.wait()
-    ordered[...] = jnp.dot(order, ql_ref[...], preferred_element_type=F32).astype(BF16)
-    for ref, (dy, other) in zip(pieces, WEIGHT_PIECES, strict=True):
-        weight[pl.ds(weight_row(place_ref, dy, other), 192), :] = ref[...]
-    fetch_own.wait()
-    query = jnp.dot(ordered[...], weight[...], preferred_element_type=F32).astype(BF16)
-    fetch_absorb.wait()
+    fetches[1].wait()
+    fetches[2].wait()
+    query = jnp.dot(ql_ref[...], weight[...], preferred_element_type=F32).astype(BF16)
+    query = jnp.dot(order, query, preferred_element_type=F32).astype(BF16)
+    fetches[3].wait()
     for h in range(HEADS):
         nope = query[:, h * QDIM : h * QDIM + NOPE]
         rope = query[:, h * QDIM + NOPE : (h + 1) * QDIM]
@@ -181,16 +185,17 @@
 def project(limit, place, depth, ql, pieces, absorb):
     column = jax.ShapeDtypeStruct((ROWS, 1), F32)
     return call(
-        project_body, [limit, place], [in_hbm(ql), in_hbm(pieces[0]), depth, *pieces[1:], in_hbm(absorb)],
+        project_body, [limit, place],
+        [in_hbm(ql), in_hbm(pieces[0]), in_hbm(depth), *pieces[1:], in_hbm(absorb)],
         [jax.ShapeDtypeStruct((NRB, HEADS, RB, WIDTH), BF16), column, column],
         [
             pltpu.VMEM((1536, HEADS * QDIM), BF16),
             pltpu.VMEM((ROWS, 1536), BF16),
-            pltpu.VMEM((ROWS, 1536), BF16),
             pltpu.VMEM((HEADS, NOPE, KVR), BF16),
-            pltpu.SemaphoreType.DMA((3,)),
+            pltpu.VMEM((1, ROWS), jnp.int32),
+            pltpu.SemaphoreType.DMA((4,)),
         ],
-        2 * ROWS * 1536 * (768 + ROWS) + 2 * ROWS * HEADS * NOPE * KVR, 24 << 20, (0, 1, len(pieces) + 2),
+        2 * ROWS * 768 * (1536 + ROWS) + 2 * ROWS * HEADS * NOPE * KVR, 24 << 20, (0, 1, 2, len(pieces) + 2),
     )
 
 

time: 71.9 us -> 71.9 us (level)
  waiting for transfers between devices: 25.1 us -> 26.8 us
  Pallas kernels: 19.2 us -> 18.1 us
    ppermute x19, waiting for transfers between devices: 25.1 us -> 26.8 us  [send(): lax.ppermute(value, axis, [(i, (i + step) % size) for i in range(size)])]
    pallas_call x5, Pallas kernels: 19.2 us -> 18.1 us  [call(): pl.pallas_call(body, in_specs=[SMEM] * len(smem) + [HBM if i in far else...]
    unnamed x6 -> x4, local copies, waits for them, and re-layouts: 1.52 us -> 0.83 us
  transfers between devices with their start and end apart: 19 -> 19, of which waited for: 8 -> 8; matrix products, arithmetic and copies ran while one was open for 0% -> 0% of each run, Pallas kernels for 8% -> 7%
where the time goes in v1:
time: 71.9 us; the launch traced here: 71.7 us
  waiting for transfers between devices  26.8 us (37%)
  starting transfers between devices  25.1 us (35%)
  Pallas kernels  18.1 us (25%)
  local copies, waits for them, and re-layouts  0.83 us (1%)
  between operations  0.72 us (1%)
    ppermute x19, waiting for transfers between devices, send(): lax.ppermute(value, axis, [(i, (i + step) % size) for i in range(size)])  26.8 us
    ppermute x19, starting transfers between devices, send(): lax.ppermute(value, axis, [(i, (i + step) % size) for i in range(size)])  25.1 us
    pallas_call x5, Pallas kernels, call(): pl.pallas_call(body, in_specs=[SMEM] * len(smem) + [HBM if i in far else...  18.1 us
  transfers between devices with their start and end apart: 19, of which 8 were waited for; matrix products, arithmetic and copies ran while one was open for 0% of the time, Pallas kernels for 7%

profile of v1, /device:TPU:64, one launch (start us, length us, event | category | flops | bytes accessed | tf_op | source)
XLA Modules:
  0.0 71.7 jit_solution(5490987439656181248)
XLA Ops:
  0.0 1.6 %collective-permute-start = (bf16[192,768]{1,0:T(8,128)(2,1)}, bf16[192,768]{1,0:T(8,128)(2,1)S(1)}, u32[]{:S(2)}, u32[]{:S(2)}) collective-permute-start(bf16[192,768]{1,0:T(8,128)(2,1)} %own_hbm.1), channel_id=1, source_target_pairs={{0,64},{64,128},{128,192},{192,0},{1,65},{65,129},{129,193},{193,1... | collective-permute-start | bytes 884744 | tf_op jit(solution)/shard_map/ppermute | solution.py:226
  1.6 1.7 %collective-permute-start.1 = (bf16[192,768]{1,0:T(8,128)(2,1)}, bf16[192,768]{1,0:T(8,128)(2,1)S(1)}, u32[]{:S(2)}, u32[]{:S(2)}) collective-permute-start(bf16[192,768]{1,0:T(8,128)(2,1)} %own_hbm.1), channel_id=1, source_target_pairs={{0,192},{64,0},{128,64},{192,128},{1,193},{65,1},{129,65},{193,129... | collective-permute-start | bytes 884744 | tf_op jit(solution)/shard_map/ppermute | solution.py:226
  3.2 7.0 %collective-permute-done.refs_0_ = bf16[192,768]{1,0:T(8,128)(2,1)S(1)} collective-permute-done((bf16[192,768]{1,0:T(8,128)(2,1)}, bf16[192,768]{1,0:T(8,128)(2,1)S(1)}, u32[]{:S(2)}, u32[]{:S(2)}) %collective-permute-start) | collective-permute-done | bytes 294944 | tf_op jit(solution)/shard_map/ppermute | solution.py:226
  10.2 0.3 collective-permute-start.2
  10.5 0.0 collective-permute-start.3
  10.5 1.9 %collective-permute-start.7 = (bf16[48,576]{1,0:T(8,128)(2,1)}, bf16[48,576]{1,0:T(8,128)(2,1)S(1)}, u32[]{:S(2)}, u32[]{:S(2)}) collective-permute-start(bf16[48,576]{1,0:T(8,128)(2,1)} %bitcast.6), channel_id=1, source_target_pairs={{0,4},{4,8},{8,12},{12,16},{16,20},{20,24},{24,28},{28,0},{1,5},{5... | collective-permute-start | bytes 165896 | tf_op jit(solution)/shard_map/ppermute | solution.py:226
  12.5 0.1 collective-permute-start.8
  12.6 2.6 %collective-permute-done.7.refs_1_.refs_0_ = bf16[48,576]{1,0:T(8,128)(2,1)S(1)} collective-permute-done((bf16[48,576]{1,0:T(8,128)(2,1)}, bf16[48,576]{1,0:T(8,128)(2,1)S(1)}, u32[]{:S(2)}, u32[]{:S(2)}) %collective-permute-start.7) | collective-permute-done | bytes 55328 | tf_op jit(solution)/shard_map/ppermute | solution.py:226
  15.2 5.7 %collective-permute-start.9 = (bf16[48,576]{1,0:T(8,128)(2,1)}, bf16[48,576]{1,0:T(8,128)(2,1)S(1)}, u32[]{:S(2)}, u32[]{:S(2)}) collective-permute-start(bf16[48,576]{1,0:T(8,128)(2,1)} %bitcast.8), channel_id=1, source_target_pairs={{0,8},{4,12},{8,16},{12,20},{16,24},{20,28},{24,0},{28,4},{1,9},{5... | collective-permute-start | bytes 165896 | tf_op jit(solution)/shard_map/ppermute | solution.py:226
  20.9 2.2 %collective-permute-done.9.refs_3_.refs_1_ = bf16[48,576]{1,0:T(8,128)(2,1)S(1)} collective-permute-done((bf16[48,576]{1,0:T(8,128)(2,1)}, bf16[48,576]{1,0:T(8,128)(2,1)S(1)}, u32[]{:S(2)}, u32[]{:S(2)}) %collective-permute-start.9) | collective-permute-done | bytes 55328 | tf_op jit(solution)/shard_map/ppermute | solution.py:226
  23.0 3.1 %collective-permute-start.14 = (bf16[48,576]{1,0:T(8,128)(2,1)S(1)}, bf16[48,576]{1,0:T(8,128)(2,1)S(1)}, u32[]{:S(2)}, u32[]{:S(2)}) collective-permute-start(bf16[48,576]{1,0:T(8,128)(2,1)S(1)} %collective-permute-done.8.refs_2_), channel_id=1, source_target_pairs={{0,24},{4,28},{8,0},{12,4},{16,8},{20,12},{24,16},{28,20},{1,25},{... | collective-permute-start | bytes 165896 | tf_op jit(solution)/shard_map/ppermute | solution.py:226
  26.1 3.4 %collective-permute-done.10.refs_4_ = bf16[48,576]{1,0:T(8,128)(2,1)S(1)} collective-permute-done((bf16[48,576]{1,0:T(8,128)(2,1)}, bf16[48,576]{1,0:T(8,128)(2,1)S(1)}, u32[]{:S(2)}, u32[]{:S(2)}) %collective-permute-start.10) | collective-permute-done | bytes 55328 | tf_op jit(solution)/shard_map/ppermute | solution.py:226
  29.5 0.0 collective-permute-start.15
  29.5 0.8 %copy-done = bf16[1,48,576]{2,1,0:T(8,128)(2,1)S(1)} copy-done((bf16[1,48,576]{2,1,0:T(8,128)(2,1)S(1)}, bf16[1,48,576]{2,1,0:T(8,128)(2,1)}, u32[]{:S(2)}) %copy-start) | copy-done | bytes 55320
  30.3 0.2 collective-permute-done.14.refs_0_
  30.5 1.5 %collective-permute-start.11 = (bf16[240,576]{1,0:T(8,128)(2,1)S(1)}, bf16[240,576]{1,0:T(8,128)(2,1)S(1)}, u32[]{:S(2)}, u32[]{:S(2)}) collective-permute-start(bf16[240,576]{1,0:T(8,128)(2,1)S(1)} %shard_map.74.refs_5_), channel_id=1, source_target_pairs={{0,1},{1,2},{2,3},{3,0},{4,5},{5,6},{6,7},{7,4},{8,9},{9,10},{10,1... | collective-permute-start | bytes 829448 | tf_op jit(solution)/shard_map/ppermute | solution.py:226
  32.0 4.0 %collective-permute-done.15.refs_1_ = bf16[96,576]{1,0:T(8,128)(2,1)S(1)} collective-permute-done((bf16[96,576]{1,0:T(8,128)(2,1)S(1)}, bf16[96,576]{1,0:T(8,128)(2,1)S(1)}, u32[]{:S(2)}, u32[]{:S(2)}) %collective-permute-start.15) | collective-permute-done | bytes 110624 | tf_op jit(solution)/shard_map/ppermute | solution.py:226
  36.0 0.0 collective-permute-done.1.refs_1_
  36.0 0.5 collective-permute-start.5
  36.5 0.0 collective-permute-done.2.refs_2_
  36.5 0.1 collective-permute-start.6
  36.6 0.0 collective-permute-done.3.refs_3_
  36.6 2.8 %collective-permute-start.17 = (bf16[144,576]{1,0:T(8,128)(2,1)S(1)}, bf16[144,576]{1,0:T(8,128)(2,1)S(1)}, u32[]{:S(2)}, u32[]{:S(2)}) collective-permute-start(bf16[144,576]{1,0:T(8,128)(2,1)S(1)} %shard_map.76.refs_9_), channel_id=1, source_target_pairs={{0,3},{1,0},{2,1},{3,2},{4,7},{5,4},{6,5},{7,6},{8,11},{9,8},{10,9... | collective-permute-start | bytes 497672 | tf_op jit(solution)/shard_map/ppermute | solution.py:226
  40.1 1.4 %collective-permute-start.12 = (bf16[240,576]{1,0:T(8,128)(2,1)S(1)}, bf16[240,576]{1,0:T(8,128)(2,1)S(1)}, u32[]{:S(2)}, u32[]{:S(2)}) collective-permute-start(bf16[240,576]{1,0:T(8,128)(2,1)S(1)} %shard_map.74.refs_5_), channel_id=1, source_target_pairs={{0,3},{1,0},{2,1},{3,2},{4,7},{5,4},{6,5},{7,6},{8,11},{9,8},{10,9... | collective-permute-start | bytes 829448 | tf_op jit(solution)/shard_map/ppermute | solution.py:226
  41.5 3.0 %collective-permute-done.17.refs_11_ = bf16[144,576]{1,0:T(8,128)(2,1)S(1)} collective-permute-done((bf16[144,576]{1,0:T(8,128)(2,1)S(1)}, bf16[144,576]{1,0:T(8,128)(2,1)S(1)}, u32[]{:S(2)}, u32[]{:S(2)}) %collective-permute-start.17) | collective-permute-done | bytes 165920 | tf_op jit(solution)/shard_map/ppermute | solution.py:226
  44.5 1.2 %collective-permute-start.13 = (bf16[240,576]{1,0:T(8,128)(2,1)S(1)}, bf16[240,576]{1,0:T(8,128)(2,1)S(1)}, u32[]{:S(2)}, u32[]{:S(2)}) collective-permute-start(bf16[240,576]{1,0:T(8,128)(2,1)S(1)} %collective-permute-done.11.refs_6_), channel_id=1, source_target_pairs={{0,1},{1,2},{2,3},{3,0},{4,5},{5,6},{6,7},{7,4},{8,9},{9,10},{10,1... | collective-permute-start | bytes 829448 | tf_op jit(solution)/shard_map/ppermute | solution.py:226
  45.7 0.1 pad_add_fusion.place_ref.refs_0_
  45.8 1.5 %collective-permute-start.16 = (bf16[144,576]{1,0:T(8,128)(2,1)S(1)}, bf16[144,576]{1,0:T(8,128)(2,1)S(1)}, u32[]{:S(2)}, u32[]{:S(2)}) collective-permute-start(bf16[144,576]{1,0:T(8,128)(2,1)S(1)} %shard_map.76.refs_9_), channel_id=1, source_target_pairs={{0,1},{1,2},{2,3},{3,0},{4,5},{5,6},{6,7},{7,4},{8,9},{9,10},{10,1... | collective-permute-start | bytes 497672 | tf_op jit(solution)/shard_map/ppermute | solution.py:226
  47.3 1.7 %collective-permute-start.18 = (bf16[144,576]{1,0:T(8,128)(2,1)S(1)}, bf16[144,576]{1,0:T(8,128)(2,1)S(1)}, u32[]{:S(2)}, u32[]{:S(2)}) collective-permute-start(bf16[144,576]{1,0:T(8,128)(2,1)S(1)} %collective-permute-done.17.refs_11_), channel_id=1, source_target_pairs={{0,3},{1,0},{2,1},{3,2},{4,7},{5,4},{6,5},{7,6},{8,11},{9,8},{10,9... | collective-permute-start | bytes 497672 | tf_op jit(solution)/shard_map/ppermute | solution.py:226
  49.0 5.0 %shard_map.73 = (bf16[4,4,128,576]{3,2,1,0:T(8,128)(2,1)S(1)}, f32[512,1]{1,0:T(8,128)S(1)}, f32[512,1]{1,0:T(8,128)S(1)}) custom-call(s32[1]{0:T(128)S(6)} %copy.8.limit_ref, s32[4]{0:T(128)S(1)} %pad_add_fusion.place_ref.refs_0_, bf16[512,1536]{1,0:T(8,128)(2,1)} %ql_hbm.1, bf16[192,768]{1,0:T(8,128)(2,1)} %own_hbm.1, s32[1,512]{1,0:T(1,128)} %bitcast.11, ...), custom_call_target="tpu_custom_call" | custom-call | flops 1879048192 | bytes 1048576 | tf_op jit(solution)/shard_map/pallas_call | solution.py:170
  54.0 4.6 %collective-permute-done.16.refs_10_ = bf16[144,576]{1,0:T(8,128)(2,1)S(1)} collective-permute-done((bf16[144,576]{1,0:T(8,128)(2,1)S(1)}, bf16[144,576]{1,0:T(8,128)(2,1)S(1)}, u32[]{:S(2)}, u32[]{:S(2)}) %collective-permute-start.16) | collective-permute-done | bytes 165920 | tf_op jit(solution)/shard_map/ppermute | solution.py:226
  58.6 13.1 %shard_map.77 = bf16[512,512]{1,0:T(8,128)(2,1)} custom-call(s32[4]{0:T(128)S(1)} %pad_add_fusion.place_ref.refs_0_, bf16[4,4,128,576]{3,2,1,0:T(8,128)(2,1)S(1)} %get-tuple-element.8.refs_1_, f32[512,1]{1,0:T(8,128)S(1)} %get-tuple-element.9.refs_2_, f32[512,1]{1,0:T(8,128)S(1)} %get-tuple-element.10.refs_3_, bf16[4,512,128]{2,1,0:T(8,128)(2,1)S(1)} %copy-done.1, ...), custom_call_target="tpu_custom_call" | custom-call | flops 6845104128 | bytes 1048576 | tf_op jit(solution)/shard_map/pallas_call | solution.py:170
  (16 shorter events, 0.1 us)
Async XLA Ops:
  0.0 10.2 %collective-permute-start = (bf16[192,768]{1,0:T(8,128)(2,1)}, bf16[192,768]{1,0:T(8,128)(2,1)S(1)}, u32[]{:S(2)}, u32[]{:S(2)}) collective-permute-start(bf16[192,768]{1,0:T(8,128)(2,1)} %own_hbm.1), channel_id=1, source_target_pairs={{0,64},{64,128},{128,192},{192,0},{1,65},{65,129},{129,193},{193,1... | collective-permute-start | bytes 884744 | tf_op jit(solution)/shard_map/ppermute | solution.py:226
  1.6 34.4 %collective-permute-start.1 = (bf16[192,768]{1,0:T(8,128)(2,1)}, bf16[192,768]{1,0:T(8,128)(2,1)S(1)}, u32[]{:S(2)}, u32[]{:S(2)}) collective-permute-start(bf16[192,768]{1,0:T(8,128)(2,1)} %own_hbm.1), channel_id=1, source_target_pairs={{0,192},{64,0},{128,64},{192,128},{1,193},{65,1},{129,65},{193,129... | collective-permute-start | bytes 884744 | tf_op jit(solution)/shard_map/ppermute | solution.py:226
  10.2 26.3 %collective-permute-start.2 = (bf16[192,768]{1,0:T(8,128)(2,1)S(1)}, bf16[192,768]{1,0:T(8,128)(2,1)S(1)}, u32[]{:S(2)}, u32[]{:S(2)}) collective-permute-start(bf16[192,768]{1,0:T(8,128)(2,1)S(1)} %collective-permute-done.refs_0_), channel_id=1, source_target_pairs={{0,64},{64,128},{128,192},{192,0},{1,65},{65,129},{129,193},{193,1... | collective-permute-start | bytes 884744 | tf_op jit(solution)/shard_map/ppermute | solution.py:226
  10.5 26.1 %collective-permute-start.3 = (bf16[192,768]{1,0:T(8,128)(2,1)}, bf16[192,768]{1,0:T(8,128)(2,1)S(1)}, u32[]{:S(2)}, u32[]{:S(2)}) collective-permute-start(bf16[192,768]{1,0:T(8,128)(2,1)} %own_hbm.1), channel_id=1, source_target_pairs={{0,32},{32,0},{1,33},{33,1},{2,34},{34,2},{3,35},{35,3},{4,36},{36... | collective-permute-start | bytes 884744 | tf_op jit(solution)/shard_map/ppermute | solution.py:226
  10.5 4.6 %collective-permute-start.7 = (bf16[48,576]{1,0:T(8,128)(2,1)}, bf16[48,576]{1,0:T(8,128)(2,1)S(1)}, u32[]{:S(2)}, u32[]{:S(2)}) collective-permute-start(bf16[48,576]{1,0:T(8,128)(2,1)} %bitcast.6), channel_id=1, source_target_pairs={{0,4},{4,8},{8,12},{12,16},{16,20},{20,24},{24,28},{28,0},{1,5},{5... | collective-permute-start | bytes 165896 | tf_op jit(solution)/shard_map/ppermute | solution.py:226
  12.5 8.4 %collective-permute-start.8 = (bf16[48,576]{1,0:T(8,128)(2,1)}, bf16[48,576]{1,0:T(8,128)(2,1)S(1)}, u32[]{:S(2)}, u32[]{:S(2)}) collective-permute-start(bf16[48,576]{1,0:T(8,128)(2,1)} %bitcast.7), channel_id=1, source_target_pairs={{0,28},{4,0},{8,4},{12,8},{16,12},{20,16},{24,20},{28,24},{1,29},{... | collective-permute-start | bytes 165896 | tf_op jit(solution)/shard_map/ppermute | solution.py:226
  15.2 7.9 %collective-permute-start.9 = (bf16[48,576]{1,0:T(8,128)(2,1)}, bf16[48,576]{1,0:T(8,128)(2,1)S(1)}, u32[]{:S(2)}, u32[]{:S(2)}) collective-permute-start(bf16[48,576]{1,0:T(8,128)(2,1)} %bitcast.8), channel_id=1, source_target_pairs={{0,8},{4,12},{8,16},{12,20},{16,24},{20,28},{24,0},{28,4},{1,9},{5... | collective-permute-start | bytes 165896 | tf_op jit(solution)/shard_map/ppermute | solution.py:226
  20.9 8.6 %collective-permute-start.10 = (bf16[48,576]{1,0:T(8,128)(2,1)}, bf16[48,576]{1,0:T(8,128)(2,1)S(1)}, u32[]{:S(2)}, u32[]{:S(2)}) collective-permute-start(bf16[48,576]{1,0:T(8,128)(2,1)} %bitcast.9), channel_id=1, source_target_pairs={{0,24},{4,28},{8,0},{12,4},{16,8},{20,12},{24,16},{28,20},{1,25},{... | collective-permute-start | bytes 165896 | tf_op jit(solution)/shard_map/ppermute | solution.py:226
  23.0 7.5 %collective-permute-start.14 = (bf16[48,576]{1,0:T(8,128)(2,1)S(1)}, bf16[48,576]{1,0:T(8,128)(2,1)S(1)}, u32[]{:S(2)}, u32[]{:S(2)}) collective-permute-start(bf16[48,576]{1,0:T(8,128)(2,1)S(1)} %collective-permute-done.8.refs_2_), channel_id=1, source_target_pairs={{0,24},{4,28},{8,0},{12,4},{16,8},{20,12},{24,16},{28,20},{1,25},{... | collective-permute-start | bytes 165896 | tf_op jit(solution)/shard_map/ppermute | solution.py:226
  29.5 6.5 %collective-permute-start.15 = (bf16[96,576]{1,0:T(8,128)(2,1)S(1)}, bf16[96,576]{1,0:T(8,128)(2,1)S(1)}, u32[]{:S(2)}, u32[]{:S(2)}) collective-permute-start(bf16[96,576]{1,0:T(8,128)(2,1)S(1)} %shard_map.75), channel_id=1, source_target_pairs={{0,8},{4,12},{8,16},{12,20},{16,24},{20,28},{24,0},{28,4},{1,9},{5... | collective-permute-start | bytes 331784 | tf_op jit(solution)/shard_map/ppermute | solution.py:226
  29.5 0.8 %copy-start = (bf16[1,48,576]{2,1,0:T(8,128)(2,1)S(1)}, bf16[1,48,576]{2,1,0:T(8,128)(2,1)}, u32[]{:S(2)}) copy-start(bf16[1,48,576]{2,1,0:T(8,128)(2,1)} %param.11) | copy-start | bytes 165892
  30.5 9.6 %collective-permute-start.11 = (bf16[240,576]{1,0:T(8,128)(2,1)S(1)}, bf16[240,576]{1,0:T(8,128)(2,1)S(1)}, u32[]{:S(2)}, u32[]{:S(2)}) collective-permute-start(bf16[240,576]{1,0:T(8,128)(2,1)S(1)} %shard_map.74.refs_5_), channel_id=1, source_target_pairs={{0,1},{1,2},{2,3},{3,0},{4,5},{5,6},{6,7},{7,4},{8,9},{9,10},{10,1... | collective-permute-start | bytes 829448 | tf_op jit(solution)/shard_map/ppermute | solution.py:226
  36.0 9.8 %collective-permute-start.4 = (bf16[192,768]{1,0:T(8,128)(2,1)S(1)}, bf16[192,768]{1,0:T(8,128)(2,1)S(1)}, u32[]{:S(2)}, u32[]{:S(2)}) collective-permute-start(bf16[192,768]{1,0:T(8,128)(2,1)S(1)} %collective-permute-done.refs_0_), channel_id=1, source_target_pairs={{0,32},{32,0},{1,33},{33,1},{2,34},{34,2},{3,35},{35,3},{4,36},{36... | collective-permute-start | bytes 884744 | tf_op jit(solution)/shard_map/ppermute | solution.py:226
  36.0 11.3 %collective-permute-start.5 = (bf16[192,768]{1,0:T(8,128)(2,1)S(1)}, bf16[192,768]{1,0:T(8,128)(2,1)S(1)}, u32[]{:S(2)}, u32[]{:S(2)}) collective-permute-start(bf16[192,768]{1,0:T(8,128)(2,1)S(1)} %collective-permute-done.1.refs_1_), channel_id=1, source_target_pairs={{0,32},{32,0},{1,33},{33,1},{2,34},{34,2},{3,35},{35,3},{4,36},{36... | collective-permute-start | bytes 884744 | tf_op jit(solution)/shard_map/ppermute | solution.py:226
  36.5 12.5 %collective-permute-start.6 = (bf16[192,768]{1,0:T(8,128)(2,1)S(1)}, bf16[192,768]{1,0:T(8,128)(2,1)S(1)}, u32[]{:S(2)}, u32[]{:S(2)}) collective-permute-start(bf16[192,768]{1,0:T(8,128)(2,1)S(1)} %collective-permute-done.2.refs_2_), channel_id=1, source_target_pairs={{0,32},{32,0},{1,33},{33,1},{2,34},{34,2},{3,35},{35,3},{4,36},{36... | collective-permute-start | bytes 884744 | tf_op jit(solution)/shard_map/ppermute | solution.py:226
  36.6 7.9 %collective-permute-start.17 = (bf16[144,576]{1,0:T(8,128)(2,1)S(1)}, bf16[144,576]{1,0:T(8,128)(2,1)S(1)}, u32[]{:S(2)}, u32[]{:S(2)}) collective-permute-start(bf16[144,576]{1,0:T(8,128)(2,1)S(1)} %shard_map.76.refs_9_), channel_id=1, source_target_pairs={{0,3},{1,0},{2,1},{3,2},{4,7},{5,4},{6,5},{7,6},{8,11},{9,8},{10,9... | collective-permute-start | bytes 497672 | tf_op jit(solution)/shard_map/ppermute | solution.py:226
  40.1 13.9 %collective-permute-start.12 = (bf16[240,576]{1,0:T(8,128)(2,1)S(1)}, bf16[240,576]{1,0:T(8,128)(2,1)S(1)}, u32[]{:S(2)}, u32[]{:S(2)}) collective-permute-start(bf16[240,576]{1,0:T(8,128)(2,1)S(1)} %shard_map.74.refs_5_), channel_id=1, source_target_pairs={{0,3},{1,0},{2,1},{3,2},{4,7},{5,4},{6,5},{7,6},{8,11},{9,8},{10,9... | collective-permute-start | bytes 829448 | tf_op jit(solution)/shard_map/ppermute | solution.py:226
  44.5 14.1 %collective-permute-start.13 = (bf16[240,576]{1,0:T(8,128)(2,1)S(1)}, bf16[240,576]{1,0:T(8,128)(2,1)S(1)}, u32[]{:S(2)}, u32[]{:S(2)}) collective-permute-start(bf16[240,576]{1,0:T(8,128)(2,1)S(1)} %collective-permute-done.11.refs_6_), channel_id=1, source_target_pairs={{0,1},{1,2},{2,3},{3,0},{4,5},{5,6},{6,7},{7,4},{8,9},{9,10},{10,1... | collective-permute-start | bytes 829448 | tf_op jit(solution)/shard_map/ppermute | solution.py:226
  45.8 12.8 %collective-permute-start.16 = (bf16[144,576]{1,0:T(8,128)(2,1)S(1)}, bf16[144,576]{1,0:T(8,128)(2,1)S(1)}, u32[]{:S(2)}, u32[]{:S(2)}) collective-permute-start(bf16[144,576]{1,0:T(8,128)(2,1)S(1)} %shard_map.76.refs_9_), channel_id=1, source_target_pairs={{0,1},{1,2},{2,3},{3,0},{4,5},{5,6},{6,7},{7,4},{8,9},{9,10},{10,1... | collective-permute-start | bytes 497672 | tf_op jit(solution)/shard_map/ppermute | solution.py:226
  47.3 11.3 %collective-permute-start.18 = (bf16[144,576]{1,0:T(8,128)(2,1)S(1)}, bf16[144,576]{1,0:T(8,128)(2,1)S(1)}, u32[]{:S(2)}, u32[]{:S(2)}) collective-permute-start(bf16[144,576]{1,0:T(8,128)(2,1)S(1)} %collective-permute-done.17.refs_11_), channel_id=1, source_target_pairs={{0,3},{1,0},{2,1},{3,2},{4,7},{5,4},{6,5},{7,6},{8,11},{9,8},{10,9... | collective-permute-start | bytes 497672 | tf_op jit(solution)/shard_map/ppermute | solution.py:226
  49.0 9.5 %copy-start.1 = (bf16[4,512,128]{2,1,0:T(8,128)(2,1)S(1)}, bf16[4,512,128]{2,1,0:T(8,128)(2,1)}, u32[]{:S(2)}) copy-start(bf16[4,512,128]{2,1,0:T(8,128)(2,1)} %refs_4_.1) | copy-start | bytes 1572868
